TPU v7x, 32 devices: a whole 2x2x4 slice. The times are simulated.
32 devices in a mesh: row: 4 (over x, core), col: 8 (over z, y).
Axes of the slice: x: 2, y: 2, z: 4, core: 2. Of those that a mesh axis runs over, the one named last changes fastest.
Arguments:
- ancestor_order: int32 [2, 48], replicated, may hold values from 0 to 47, each once within a row
- factor_rows: bfloat16 [2, 24576, 512], P(None, ('row', 'col')), may hold values from -0.0390625 to 0.0390625
- factor_inverse: bfloat16 [2, 512, 512], replicated
- ancestor_inverse: bfloat16 [24576, 24576], P('col', 'row'), may hold values from -6 to 6
- diagonal_inverse: float32 [2, 512, 512], P(None, None, 'row'), may hold values from -6 to 6
Outputs:
- offdiag_inverse: bfloat16 [2, 24576, 512], P(None, 'col', 'row')
- diag_updated: float32 [2, 512, 512], P(None, None, 'row')
Inputs may be any that keep to these rules, and one draw needn't show every extreme that they name: `ancestor_order`: each row lists every ancestor block once; its first 40 entries are the blocks coupled to that supernode.
All inputs are finite; a program needn't handle non-finite values.
Results may differ from a plain program's by a relative error of at most 0.011.
Values may be sent and summed in bfloat16 or wider, within the bound.
A program may use at most 128 MiB of HBM per device.

v0:
```python
import jax
import jax.numpy as jnp
from jax import lax
from jax.sharding import PartitionSpec as P

NSEL = 40


def broadcast(value, axis, source):
    kept = jnp.where(lax.axis_index(axis) == source, value, 0).astype(value.dtype)
    return lax.psum(kept, axis)


def process(listing, pieces, factor_inv, inverse_block, diag_inv):
    piece_rows = pieces.shape[1]
    block_width = pieces.shape[2]
    row_count = lax.axis_size("row")
    col_count = lax.axis_size("col")
    row_index = lax.axis_index("row")
    col_index = lax.axis_index("col")
    chosen = listing[:, :NSEL]
    first_row = (row_index * col_count + col_index) * piece_rows
    own_labels = (first_row + jnp.arange(piece_rows, dtype=jnp.int32)) // block_width
    own_keep = jnp.any(chosen[:, :, None] == own_labels[None, None, :], axis=1).astype(jnp.float32)
    normed = jnp.einsum("srk,skj->srj", pieces, factor_inv, preferred_element_type=jnp.float32)
    normed = (normed * own_keep[:, :, None]).astype(jnp.bfloat16)
    row_panel = lax.all_gather(normed, "col", axis=1, tiled=True)
    column_rows = inverse_block.shape[0]
    per_row = col_count // row_count
    offset = col_index % per_row * column_rows
    column_part = lax.dynamic_slice_in_dim(row_panel, offset, column_rows, 1)
    columns = broadcast(column_part, "row", col_index // per_row)
    partial_value = jnp.einsum(
        "pq,sqj->spj", inverse_block, row_panel, preferred_element_type=jnp.float32
    )
    lifted = columns.astype(jnp.float32)
    shares = lax.psum_scatter(partial_value, "row", scatter_dimension=2, tiled=True)
    local_terms = jnp.einsum("spk,spj->skj", lifted, shares, precision=lax.Precision.HIGHEST)
    correction = lax.psum(local_terms.astype(jnp.bfloat16), "col").astype(jnp.float32)
    col_labels = (col_index * column_rows + jnp.arange(column_rows, dtype=jnp.int32)) // block_width
    col_keep = jnp.any(chosen[:, :, None] == col_labels[None, None, :], axis=1).astype(jnp.float32)
    offdiag = (-(shares * col_keep[:, :, None])).astype(jnp.bfloat16)
    return (offdiag, diag_inv + correction)


def body(ancestor_order, factor_rows, factor_inverse, ancestor_inverse, diagonal_inverse):
    return process(ancestor_order, factor_rows, factor_inverse, ancestor_inverse, diagonal_inverse)


def solution(mesh):
    placed = (P(), P(None, ("row", "col"), None), P(), P("col", "row"), P(None, None, "row"))
    return jax.shard_map(
        body,
        mesh=mesh,
        in_specs=placed,
        out_specs=(P(None, "col", "row"), P(None, None, "row")),
        check_vma=False,
    )
```

profile of v0, /device:TPU:0, one launch (start us, length us, event | category | flops | bytes accessed | tf_op | source)
XLA Modules:
  0.0 507.6 jit_solution(1334670819939079602)
XLA Ops:
  7.2 0.0 copy-start
  7.2 0.0 all-gather.2.cloned.1.call-start
  7.3 0.9 compare_reduce_fusion.1
  8.2 0.4 copy-done
  8.6 3.3 multiply_convert_fusion
  11.9 0.0 all-gather.2.cloned.1.call-update
  12.0 0.0 all-reduce.3.cloned.1.call-start
  12.0 178.9 %all-gather.2.cloned.1.call-done = bf16[2,6144,512]{2,1,0:T(8,128)(2,1)} async-done(((bf16[2,768,512]{2,1,0:T(8,128)(2,1)}), bf16[2,6144,512]{2,1,0:T(8,128)(2,1)}) %all-gather.2.cloned.1.call-update) | async-done | bytes 12582928 | tf_op jit(solution)/shard_map/all_gather | solution.py:27
  190.9 6.6 %dynamic-slice_select_fusion = bf16[2,3072,512]{2,1,0:T(8,128)(2,1)} fusion(bf16[2,6144,512]{2,1,0:T(8,128)(2,1)} %all-gather.2.cloned.1.call-done, s32[]{:T(128)S(6)} %select_n.45, pred[]{:T(512)S(6)} %eq.37), kind=kLoop, calls=%fused_computation.3 | loop fusion | flops 3145728 | bytes 12582917 | tf_op jit(solution)/shard_map/jit(_where)/select_n | solution.py:10
  197.5 0.0 all-reduce.3.cloned.1.call-update
  197.6 0.0 reduce-scatter.2.cloned.1.call-start
  197.6 49.2 %fusion.2 = f32[2,3072,512]{1,2,0:T(8,128)} fusion(bf16[2,6144,512]{2,1,0:T(8,128)(2,1)} %all-gather.2.cloned.1.call-done, bf16[3072,6144]{1,0:T(8,128)(2,1)} %param.8), kind=kOutput, calls=%fused_computation.2 | convolution fusion | flops 38654705664 | bytes 62914560 | tf_op jit(solution)/shard_map/pq,sqj->spj/dot_general | solution.py:33
  246.9 0.0 copy-start.2
  246.9 0.0 reduce-scatter.2.cloned.1.call-update
  246.9 0.2 all-reduce.5.cloned.1.call-start
  247.1 0.4 copy-done.2
  247.5 0.2 compare_reduce_fusion
  247.8 67.7 %all-reduce.3.cloned.1.call-done = bf16[2,3072,512]{2,1,0:T(8,128)(2,1)} async-done(((bf16[2,3072,512]{2,1,0:T(8,128)(2,1)}), bf16[2,3072,512]{2,1,0:T(8,128)(2,1)}) %all-reduce.3.cloned.1.call-update) | async-done | bytes 6291472 | tf_op jit(solution)/shard_map/psum | solution.py:11
  315.5 102.4 %reduce-scatter.2.cloned.1.call-done = f32[2,3072,128]{1,2,0:T(8,128)} async-done(((f32[2,3072,512]{1,2,0:T(8,128)}), f32[2,3072,128]{1,2,0:T(8,128)}) %reduce-scatter.2.cloned.1.call-update) | async-done | bytes 3145744 | tf_op jit(solution)/shard_map/reduce_scatter | solution.py:37
  417.9 10.1 %convolution_convert_fusion = bf16[2,512,128]{2,1,0:T(8,128)(2,1)} fusion(bf16[2,3072,512]{2,1,0:T(8,128)(2,1)} %all-reduce.3.cloned.1.call-done, f32[2,3072,128]{1,2,0:T(8,128)} %reduce-scatter.2.cloned.1.call-done), kind=kOutput, calls=%fused_computation.6 | convolution fusion | flops 4831969280 | bytes 9699328 | tf_op jit(solution)/shard_map/spk,spj->skj/dot_general | solution.py:38
  428.0 0.0 all-reduce.5.cloned.1.call-update
  428.0 0.0 copy-start.1
  428.0 2.3 negate_convert_fusion
  430.4 1.6 copy.14
  431.9 67.2 %all-reduce.5.cloned.1.call-done = bf16[2,512,128]{2,1,0:T(8,128)(2,1)} async-done(((bf16[2,512,128]{2,1,0:T(8,128)(2,1)}), bf16[2,512,128]{2,1,0:T(8,128)(2,1)}) %all-reduce.5.cloned.1.call-update) | async-done | bytes 262160 | tf_op jit(solution)/shard_map/psum | solution.py:39
  499.2 1.9 convert_add_fusion
  501.1 0.0 copy-done.1
  (4 shorter events, 0.0 us)
Async XLA Ops:
  7.2 1.4 copy-start
  7.2 183.8 %all-gather.2.cloned.1.call-start = ((), (), s32[]{:S(2)}) async-start(), calls=%async_computation.1 | async-start | bytes 14155776 | tf_op jit(solution)/shard_map/all_gather | solution.py:27
  12.0 303.5 %all-reduce.3.cloned.1.call-start = ((), (), s32[]{:S(2)}) async-start(), calls=%async_computation.3 | async-start | bytes 12582912 | tf_op jit(solution)/shard_map/psum | solution.py:11
  197.6 220.3 %reduce-scatter.2.cloned.1.call-start = ((), (), s32[]{:S(2)}) async-start(), calls=%async_computation.2 | async-start | bytes 15728640 | tf_op jit(solution)/shard_map/reduce_scatter | solution.py:37
  246.9 0.7 copy-start.2
  246.9 252.3 %all-reduce.5.cloned.1.call-start = ((), (), s32[]{:S(2)}) async-start(), calls=%async_computation.4 | async-start | bytes 524288 | tf_op jit(solution)/shard_map/psum | solution.py:39
  428.0 73.1 %copy-start.1 = (bf16[2,768,512]{2,1,0:T(8,128)(2,1)S(1)}, bf16[2,768,512]{2,1,0:T(8,128)(2,1)}, u32[]{:S(2)}) copy-start(bf16[2,768,512]{2,1,0:T(8,128)(2,1)} %param.6) | copy-start | bytes 4718596
Sparse Core Ops, SparseCore 0:
  12.1 178.8 all-gather.1
  197.7 117.7 all-reduce.2
  318.1 99.8 reduce-scatter.1
  428.1 70.9 all-reduce.4
where the time goes:
time: 508 us
  waiting for transfers between devices  416 us (82%)
  matrix products  62.6 us (12%)
  between operations  13.9 us (3%)
  other arithmetic  12 us (2%)
    all_gather x1, waiting for transfers between devices, process(): row_panel = lax.all_gather(normed, 'col', axis=1, tiled=True)  179 us
    reduce_scatter x1, waiting for transfers between devices, process(): lax.psum_scatter(partial_value, 'row', scatter_dimension=2, tiled=True)  102 us
    psum x1, waiting for transfers between devices, broadcast(): return lax.psum(kept, axis)  67.7 us
    psum x1, waiting for transfers between devices, process(): lax.psum(local_terms.astype(jnp.bfloat16), 'col').astype(jnp.float32)  67.2 us
    dot_general x1, matrix products, process(): jnp.einsum('pq,sqj->spj', inverse_block, row_panel, preferred_element_typ...  49.2 us
  transfers between devices with their start and end apart: 4, of which 4 were waited for; matrix products, arithmetic and copies ran while one was open for 11% of the time, Pallas kernels for 0%

commit v1 on v0

--- a/solution.py
+++ b/solution.py
@@ -36,7 +36,9 @@
     lifted = columns.astype(jnp.float32)
     shares = lax.psum_scatter(partial_value, "row", scatter_dimension=2, tiled=True)
     local_terms = jnp.einsum("spk,spj->skj", lifted, shares, precision=lax.Precision.HIGHEST)
-    correction = lax.psum(local_terms.astype(jnp.bfloat16), "col").astype(jnp.float32)
+    correction = jnp.sum(lax.all_gather(local_terms.astype(jnp.bfloat16), "col"), axis=0).astype(
+        jnp.float32
+    )
     col_labels = (col_index * column_rows + jnp.arange(column_rows, dtype=jnp.int32)) // block_width
     col_keep = jnp.any(chosen[:, :, None] == col_labels[None, None, :], axis=1).astype(jnp.float32)
     offdiag = (-(shares * col_keep[:, :, None])).astype(jnp.bfloat16)

time: 508 us -> 488 us (0.961)
  waiting for transfers between devices: 416 us -> 395 us
    psum x1 -> x0, waiting for transfers between devices: 67.2 us -> none  [process(): lax.psum(local_terms.astype(jnp.bfloat16), 'col').astype(jnp.float32)]
    all_gather x0 -> x1, waiting for transfers between devices: none -> 45 us  [process(): lax.all_gather(local_terms.astype(jnp.bfloat16), 'col')]
where the time goes in v1:
time: 488 us
  waiting for transfers between devices  395 us (81%)
  matrix products  62.6 us (13%)
  other arithmetic  13.9 us (3%)
  between operations  13.9 us (3%)
    all_gather x1, waiting for transfers between devices, process(): row_panel = lax.all_gather(normed, 'col', axis=1, tiled=True)  179 us
    reduce_scatter x1, waiting for transfers between devices, process(): lax.psum_scatter(partial_value, 'row', scatter_dimension=2, tiled=True)  102 us
    psum x1, waiting for transfers between devices, broadcast(): return lax.psum(kept, axis)  68.3 us
    dot_general x1, matrix products, process(): jnp.einsum('pq,sqj->spj', inverse_block, row_panel, preferred_element_typ...  49.2 us
    all_gather x1, waiting for transfers between devices, process(): lax.all_gather(local_terms.astype(jnp.bfloat16), 'col')  45 us
    dot_general x1, matrix products, process(): jnp.einsum('spk,spj->skj', lifted, shares, precision=lax.Precision.HIGHEST)  10.1 us
  transfers between devices with their start and end apart: 4, of which 4 were waited for; matrix products, arithmetic and copies ran while one was open for 11% of the time, Pallas kernels for 0%

profile of v1, /device:TPU:0, one launch (start us, length us, event | category | flops | bytes accessed | tf_op | source)
XLA Modules:
  0.0 487.6 jit_solution(4542087136023890685)
XLA Ops:
  7.2 0.0 copy-start
  7.2 0.0 all-gather.4.cloned.1.call-start
  7.3 0.9 compare_reduce_fusion.1
  8.2 0.4 copy-done
  8.6 3.3 multiply_convert_fusion
  11.9 0.0 all-gather.4.cloned.1.call-update
  12.0 0.0 all-reduce.2.cloned.1.call-start
  12.0 178.9 %all-gather.4.cloned.1.call-done = bf16[2,6144,512]{2,1,0:T(8,128)(2,1)} async-done(((bf16[2,768,512]{2,1,0:T(8,128)(2,1)}), bf16[2,6144,512]{2,1,0:T(8,128)(2,1)}) %all-gather.4.cloned.1.call-update) | async-done | bytes 12582928 | tf_op jit(solution)/shard_map/all_gather | solution.py:27
  190.9 6.6 %dynamic-slice_select_fusion = bf16[2,3072,512]{2,1,0:T(8,128)(2,1)} fusion(bf16[2,6144,512]{2,1,0:T(8,128)(2,1)} %all-gather.4.cloned.1.call-done, s32[]{:T(128)S(6)} %select_n.45, pred[]{:T(512)S(6)} %eq.37), kind=kLoop, calls=%fused_computation.3 | loop fusion | flops 3145728 | bytes 12582917 | tf_op jit(solution)/shard_map/jit(_where)/select_n | solution.py:10
  197.5 0.0 all-reduce.2.cloned.1.call-update
  197.6 0.0 reduce-scatter.2.cloned.1.call-start
  197.6 49.2 %fusion.2 = f32[2,3072,512]{1,2,0:T(8,128)} fusion(bf16[2,6144,512]{2,1,0:T(8,128)(2,1)} %all-gather.4.cloned.1.call-done, bf16[3072,6144]{1,0:T(8,128)(2,1)} %param.8), kind=kOutput, calls=%fused_computation.2 | convolution fusion | flops 38654705664 | bytes 62914560 | tf_op jit(solution)/shard_map/pq,sqj->spj/dot_general | solution.py:33
  246.9 0.0 reduce-scatter.2.cloned.1.call-update
  246.9 0.0 copy-start.2
  246.9 0.2 all-gather.6.cloned.1.call-start
  247.1 68.3 %all-reduce.2.cloned.1.call-done = bf16[2,3072,512]{2,1,0:T(8,128)(2,1)} async-done(((bf16[2,3072,512]{2,1,0:T(8,128)(2,1)}), bf16[2,3072,512]{2,1,0:T(8,128)(2,1)}) %all-reduce.2.cloned.1.call-update) | async-done | bytes 6291472 | tf_op jit(solution)/shard_map/psum | solution.py:11
  315.5 102.4 %reduce-scatter.2.cloned.1.call-done = f32[2,3072,128]{1,2,0:T(8,128)} async-done(((f32[2,3072,512]{1,2,0:T(8,128)}), f32[2,3072,128]{1,2,0:T(8,128)}) %reduce-scatter.2.cloned.1.call-update) | async-done | bytes 3145744 | tf_op jit(solution)/shard_map/reduce_scatter | solution.py:37
  417.9 10.1 %convolution_convert_fusion = bf16[2,512,128]{2,1,0:T(8,128)(2,1)} fusion(bf16[2,3072,512]{2,1,0:T(8,128)(2,1)} %all-reduce.2.cloned.1.call-done, f32[2,3072,128]{1,2,0:T(8,128)} %reduce-scatter.2.cloned.1.call-done), kind=kOutput, calls=%fused_computation.6 | convolution fusion | flops 4831969280 | bytes 9699328 | tf_op jit(solution)/shard_map/spk,spj->skj/dot_general | solution.py:38
  428.0 0.0 all-gather.6.cloned.1.call-update
  428.0 0.0 copy-done.2
  428.0 0.2 compare_reduce_fusion
  428.3 0.0 copy-start.1
  428.3 2.4 negate_convert_fusion
  430.6 1.6 copy.18
  432.2 45.0 %all-gather.6.cloned.1.call-done = bf16[16,512,128]{2,1,0:T(8,128)(2,1)} async-done(((bf16[2,512,128]{2,1,0:T(8,128)(2,1)}), bf16[16,512,128]{2,1,0:T(8,128)(2,1)}) %all-gather.6.cloned.1.call-update) | async-done | bytes 2097168 | tf_op jit(solution)/shard_map/all_gather | solution.py:39
  477.2 2.0 reduce_sum.12
  479.2 1.9 convert_add_fusion
  481.1 0.0 copy-done.1
  (4 shorter events, 0.0 us)
Async XLA Ops:
  7.2 1.4 copy-start
  7.2 183.8 %all-gather.4.cloned.1.call-start = ((), (), s32[]{:S(2)}) async-start(), calls=%async_computation.1 | async-start | bytes 14155776 | tf_op jit(solution)/shard_map/all_gather | solution.py:27
  12.0 303.5 %all-reduce.2.cloned.1.call-start = ((), (), s32[]{:S(2)}) async-start(), calls=%async_computation.3 | async-start | bytes 12582912 | tf_op jit(solution)/shard_map/psum | solution.py:11
  197.6 220.3 %reduce-scatter.2.cloned.1.call-start = ((), (), s32[]{:S(2)}) async-start(), calls=%async_computation.2 | async-start | bytes 15728640 | tf_op jit(solution)/shard_map/reduce_scatter | solution.py:37
  246.9 181.1 %copy-start.2 = (s32[2,48]{1,0:T(2,128)S(1)}, s32[2,48]{1,0:T(2,128)}, u32[]{:S(2)}) copy-start(s32[2,48]{1,0:T(2,128)} %param.5) | copy-start | bytes 1156
  246.9 230.4 %all-gather.6.cloned.1.call-start = ((), (), s32[]{:S(2)}) async-start(), calls=%async_computation.4 | async-start | bytes 2359296 | tf_op jit(solution)/shard_map/all_gather | solution.py:39
  428.3 52.8 %copy-start.1 = (bf16[2,768,512]{2,1,0:T(8,128)(2,1)S(1)}, bf16[2,768,512]{2,1,0:T(8,128)(2,1)}, u32[]{:S(2)}) copy-start(bf16[2,768,512]{2,1,0:T(8,128)(2,1)} %param.6) | copy-start | bytes 4718596
Sparse Core Ops, SparseCore 0:
  12.1 178.8 all-gather.3
  197.7 117.7 all-reduce.1
  318.1 99.8 reduce-scatter.1
  428.1 49.0 all-gather.5
